TPU v7x, 32 devices: a whole 2x2x4 slice. The times are simulated.
32 devices in a mesh: groups: 2 (over x), wide: 16 (over z, y, core).
Axes of the slice: x: 2, y: 2, z: 4, core: 2. Of those that a mesh axis runs over, the one named last changes fastest.
Arguments:
- half_integrals: float32 [256, 512, 800], P(('groups', 'wide')), parts along dimension 0, may hold values from -40 to 40
- pair_list: int32 [256, 2], P('groups'), parts along dimension 0, may hold values from 0 to 199, as said below
- occupied_energy: float32 [400], P('groups'), parts along dimension 0, may hold values from -3 to -0.3
- virtual_orbitals: float32 [1600, 600], P('groups'), parts along dimension 0, may hold values from -0.21875 to 0.21875
- tile_order: int32 [64], replicated, may hold values from 0 to 63, each once
Outputs:
- transformed: float32 [256, 512, 600], P('groups', 'wide'), parts along dimension 0
- pair_rms: float32 [256], P('groups'), parts along dimension 0
There are 2 independent parts, one for each index of `groups`. A program takes and returns all parts, laid end to end along the dimension named above; an argument that names none is the same for every part. Nothing has to cross between parts.
Inputs may be any that keep to these rules, and one draw needn't show every extreme that they name: `pair_list`: each row is a distinct pair (i, j) with i <= j.
All inputs are finite; a program needn't handle non-finite values.
Results may differ from a plain program's by a relative error of at most 0.00007.
Values sent between devices are 32-bit elements; how exact they have to be, the bound alone decides.
A program may use at most 128 MiB of HBM per device.

v0:
```python
import jax
import jax.numpy as jnp
from jax import lax
from jax.sharding import PartitionSpec as P

TILE_S = 8


def pair_weights(pair_list, occupied_energy):
    orbital = jnp.arange(occupied_energy.shape[0], dtype=jnp.int32)
    first = jnp.sum(
        jnp.where(pair_list[:, 0:1] == orbital[None, :], occupied_energy[None, :], 0.0), axis=1
    )
    second = jnp.sum(
        jnp.where(pair_list[:, 1:2] == orbital[None, :], occupied_energy[None, :], 0.0), axis=1
    )
    return jnp.exp(0.3 * (first + second))


def transform(block, virtual_orbitals, scale):
    product = jnp.einsum("psr,ra->psa", block, virtual_orbitals, precision=lax.Precision.HIGHEST)
    return product * scale[:, None, None]


def shards(half_integrals, pair_list, occupied_energy, virtual_orbitals, tile_order):
    pair_rows = half_integrals.shape[0]
    columns = half_integrals.shape[1]
    basis = half_integrals.shape[2]
    virtuals = virtual_orbitals.shape[1]
    weights = pair_weights(pair_list, occupied_energy)
    tiled = half_integrals.reshape(pair_rows, tile_order.shape[0], TILE_S, basis)
    ordered = jnp.take(tiled, tile_order, axis=1).reshape(pair_rows, columns, basis)
    own_weights = lax.dynamic_slice_in_dim(weights, lax.axis_index("wide") * pair_rows, pair_rows)
    local = transform(ordered, virtual_orbitals, own_weights)
    squares = jnp.sum(local * local, axis=(1, 2))
    transformed = lax.all_to_all(local, "wide", split_axis=1, concat_axis=0, tiled=True)
    totals = lax.all_gather(squares, "wide", axis=0, tiled=True)
    pair_rms = jnp.sqrt(totals / (columns * virtuals) + 1e-06)
    return (transformed, pair_rms)


def solution(mesh):
    in_specs = (
        P(("groups", "wide"), None, None),
        P("groups", None),
        P("groups"),
        P("groups", None),
        P(),
    )
    out_specs = (P("groups", "wide", None), P("groups"))
    return jax.shard_map(shards, mesh=mesh, in_specs=in_specs, out_specs=out_specs, check_vma=False)
```

profile of v0, /device:TPU:16, one launch (start us, length us, event | category | flops | bytes accessed | tf_op | source)
XLA Modules:
  0.0 366.4 jit_solution(15603206218613331399)
XLA Ops:
  0.6 0.0 copy-start
  0.6 0.8 compare_select_fusion
  1.5 0.7 compare_and_fusion
  2.1 0.8 slice_bitcast_fusion.1
  2.9 15.6 %copy.23 = f32[8,512,800]{2,1,0:T(8,128)} copy(f32[8,512,800]{1,2,0:T(8,128)} %param.5) | data formatting | bytes 26214400 | tf_op args[0]
  18.4 0.0 copy-start.2
  18.4 12.4 %copy.24 = f32[8,64,8,800]{3,2,0,1:T(8,128)} copy(f32[8,64,8,800]{3,2,1,0:T(8,128)} %bitcast.26) | data formatting | bytes 26214400 | tf_op jit(solution)/shard_map/reshape | solution.py:31
  30.8 0.1 broadcast_in_dim.37
  30.9 0.1 broadcast_in_dim.38
  31.0 0.0 copy-done.2
  31.0 0.1 select_reduce_fusion
  31.1 0.1 dynamic_slice.3
  31.2 11.9 %gather_fusion = f32[64,8,8,800]{3,2,1,0:T(8,128)} fusion(f32[8,64,8,800]{3,2,0,1:T(8,128)} %copy.24, s32[1024]{0:T(1024)S(1)} %pad_clamp_fusion), kind=kCustom, calls=%fused_computation | custom fusion | bytes 26214656 | tf_op jit(solution)/shard_map/jit(_take)/gather | solution.py:32
  43.1 0.0 copy-done
  43.1 37.2 %multiply_reduce_fusion = (f32[8]{0:T(128)S(1)}, f32[8,512,600]{1,2,0:T(8,128)}) fusion(f32[8]{0:T(128)S(1)} %dynamic_slice.3, f32[800,600]{1,0:T(8,128)S(1)} %copy-done, pred[512]{0:T(512)(128)(4,1)S(1)} %broadcast_in_dim.38, f32[64,8,8,800]{3,2,1,0:T(8,128)} %gather_fusion), kind=kOutput, calls=%fused_computation.4 | convolution fusion | flops 23603609600 | bytes 24858176 | tf_op jit(solution)/shard_map/psr,ra->psa/dot_general | solution.py:21
  80.3 12.3 %copy.27 = f32[8,512,600]{2,0,1:T(8,128)} copy(f32[8,512,600]{1,2,0:T(8,128)} %get-tuple-element.13) | data formatting | bytes 19660800 | tf_op jit(solution)/shard_map/mul | solution.py:22
  92.6 0.0 copy-start.3
  92.6 6.3 %all-to-all-start = ((f32[8,512,600]{2,0,1:T(8,128)}), f32[8,512,600]{2,0,1:T(8,128)}, u32[]{:S(2)}, u32[]{:S(2)}) async-start(f32[8,512,600]{2,0,1:T(8,128)} %copy.27), calls=%async_computation | async-start | bytes 20971520 | tf_op jit(solution)/shard_map/all_to_all | solution.py:36
  98.9 0.0 copy-done.3
  98.9 0.6 dynamic-slice
  100.2 0.2 dynamic-update-slice
  100.4 244.1 %all-reduce = f32[128]{0:T(128)S(1)} all-reduce(f32[128]{0:T(128)S(1)} %dynamic-update-slice), channel_id=1, replica_groups=mesh['groups'=2,'wide'=16] {'wide'}, use_global_device_ids=true, to_apply=%add | all-reduce | flops 128 | bytes 1024
  344.5 0.5 add_sqrt_fusion
  345.0 0.0 all-to-all-done
  345.0 0.0 copy-start.1
  345.0 9.8 %copy.29 = f32[16,8,32,600]{3,2,1,0:T(8,128)} copy(f32[16,8,32,600]{3,1,2,0:T(8,128)} %bitcast.8) | data formatting | bytes 19660800 | tf_op jit(solution)/shard_map/all_to_all | solution.py:36
  354.8 11.7 %copy.30 = f32[128,32,600]{0,2,1:T(8,128)} copy(f32[128,32,600]{2,1,0:T(8,128)} %bitcast.27) | data formatting | bytes 19660800
  366.4 0.0 copy-done.1
  (3 shorter events, 0.0 us)
Async XLA Ops:
  0.6 42.4 %copy-start = (f32[800,600]{1,0:T(8,128)S(1)}, f32[800,600]{1,0:T(8,128)}, u32[]{:S(2)}) copy-start(f32[800,600]{1,0:T(8,128)} %param.8) | copy-start | bytes 5760004
  18.4 12.6 %copy-start.2 = (f32[200]{0:T(256)S(1)}, f32[200]{0:T(256)}, u32[]{:S(2)}) copy-start(f32[200]{0:T(256)} %param.7) | copy-start | bytes 2404
  92.6 6.3 %copy-start.3 = (u32[32]{0:T(128)S(1)}, u32[32]{0:T(128)}, u32[]{:S(2)}) copy-start(u32[32]{0:T(128)} %constant.37) | copy-start | bytes 388
  92.6 252.4 %all-to-all-start = ((f32[8,512,600]{2,0,1:T(8,128)}), f32[8,512,600]{2,0,1:T(8,128)}, u32[]{:S(2)}, u32[]{:S(2)}) async-start(f32[8,512,600]{2,0,1:T(8,128)} %copy.27), calls=%async_computation | async-start | bytes 20971520 | tf_op jit(solution)/shard_map/all_to_all | solution.py:36
  345.0 21.4 %copy-start.1 = (f32[800,600]{1,0:T(8,128)S(1)}, f32[800,600]{1,0:T(8,128)}, u32[]{:S(2)}) copy-start(f32[800,600]{1,0:T(8,128)} %param.8) | copy-start | bytes 5760004
where the time goes:
time: 367 us; the launch traced here: 366 us
  blocking collectives  244 us (66%)
  local copies, waits for them, and re-layouts  75.4 us (21%)
  matrix products  37.2 us (10%)
  starting transfers between devices  6.32 us (2%)
    unnamed x1, blocking collectives  244 us
    dot_general x1, matrix products, transform(): jnp.einsum('psr,ra->psa', block, virtual_orbitals, precision=lax.Precisio...  37.2 us
    unnamed x13, local copies, waits for them, and re-layouts  28.1 us
    reshape x1, local copies, waits for them, and re-layouts, shards(): half_integrals.reshape(pair_rows, tile_order.shape[0], TILE_S, basis)  12.4 us
    mul x1, local copies, waits for them, and re-layouts, transform(): return product * scale[:, None, None]  12.3 us
    gather x1, local copies, waits for them, and re-layouts, shards(): jnp.take(tiled, tile_order, axis=1).reshape(pair_rows, columns, basis)  11.9 us
    all_to_all x1, local copies, waits for them, and re-layouts, shards(): lax.all_to_all(local, 'wide', split_axis=1, concat_axis=0, tiled=True)  9.78 us
  transfers between devices with their start and end apart: 1, of which 0 were waited for; matrix products, arithmetic and copies ran while one was open for 0% of the time, Pallas kernels for 0%

commit v1 on v0

v1 whole, which is shorter than its diff:
```python
import functools

import jax
import jax.numpy as jnp
from jax import lax
from jax.experimental import pallas as pl
from jax.experimental.pallas import tpu as pltpu
from jax.sharding import PartitionSpec as P

TILE_S = 8
LANES = 128
MESH = pl.DeviceIdType.MESH


def round_up(value, step):
    return (value + step - 1) // step * step


def split(value):
    high = value.astype(jnp.bfloat16)
    low = (value - high.astype(jnp.float32)).astype(jnp.bfloat16)
    return high, low


def prepare_kernel(
    order_ref, pair_ref, energy_ref, x_ref, w_ref, xs, w_high, w_low, scales,
    index_buf, turned, slot_of, sems,
):
    me = lax.axis_index("wide")
    step = pl.program_id(0)
    steps = pl.num_programs(0)
    pair_rows, basis, _ = x_ref.shape
    virtuals = w_ref.shape[1]
    deep = xs.shape[0]
    block_rows = TILE_S * pair_rows
    tiles = LANES // TILE_S
    side = lax.rem(step, 2)

    @pl.when(step == 0)
    def _():
        def invert(k, carry):
            slot_of[order_ref[k]] = k
            return carry

        lax.fori_loop(0, order_ref.shape[0], invert, 0)
        w_high[...] = jnp.zeros_like(w_high)
        w_low[...] = jnp.zeros_like(w_low)
        high, low = split(w_ref[...])
        w_high[:basis, :virtuals] = high
        w_low[:basis, :virtuals] = low
        my_rows = pl.ds(pl.multiple_of(me * pair_rows, pair_rows), pair_rows)
        orbitals = energy_ref.shape[1]
        orbital = lax.broadcasted_iota(jnp.int32, (pair_rows, orbitals), 1).astype(jnp.float32)
        energy = jnp.zeros((pair_rows, 1), jnp.float32)
        for k in range(2):
            line = pair_ref[k : k + 1, :].astype(jnp.float32)
            index_buf[...] = jnp.broadcast_to(line, (LANES, line.shape[1])).T
            hit = index_buf[my_rows, 0:1] == orbital
            energy = energy + jnp.sum(jnp.where(hit, energy_ref[...], 0.0), axis=1, keepdims=True)
        scales[...] = jnp.broadcast_to(jnp.exp(0.3 * energy), scales.shape)

    def copy(at, which, u):
        rows = pl.ds(pl.multiple_of(slot_of[at * tiles + u] * block_rows, block_rows), block_rows)
        return pltpu.make_async_copy(
            turned.at[which, :, pl.ds(u * block_rows, block_rows), :], xs.at[:, rows, :], sems.at[which, u]
        )

    @pl.when(step >= 2)
    def _():
        for u in range(tiles):
            copy(step - 2, side, u).wait()

    for p in range(pair_rows):
        for k in range(deep):
            size = min(LANES, basis - k * LANES)
            piece = x_ref[p, k * LANES : k * LANES + size, :]
            if size < LANES:
                piece = jnp.concatenate([piece, jnp.zeros((LANES - size, LANES), jnp.float32)], axis=0)
            turned[side, k, pl.ds(p, LANES, stride=pair_rows), :] = piece.T
    for u in range(tiles):
        copy(step, side, u).start()

    @pl.when(step == steps - 1)
    def _():
        for u in range(tiles):
            copy(step - 1, 1 - side, u).wait()
        for u in range(tiles):
            copy(step, side, u).wait()


def exchange_kernel(
    n, xs, w_high, w_low, scales, recv_main, recv_rest, sq_recv,
    x_buf, x_high, x_low, squares, sq_send, send_main, send_rest,
    x_sems, main_sems, rest_sems, main_recv_sems, rest_recv_sems,
    sq_sems, sq_recv_sems, own_sems,
):
    me = lax.axis_index("wide")
    _, span, pair_rows, full = send_main.shape
    rest = send_rest.shape[2] // span
    rows = span * pair_rows
    deep = xs.shape[0]
    plane = n // 4
    my_rows = pl.ds(pl.multiple_of(me * pair_rows, pair_rows), pair_rows)

    barrier = pltpu.get_barrier_semaphore()

    def greet(j, carry):
        pl.semaphore_signal(barrier, inc=1, device_id={"wide": lax.rem(me + j, n)}, device_id_type=MESH)
        return carry

    lax.fori_loop(1, n, greet, 0)

    sign = 1 - 2 * (me // (n // 2))
    my_plane = me // plane

    def place(c):
        other = lax.rem(my_plane + sign * (1 + c // plane) + 8, 4)
        return other * plane + lax.rem(me + c, plane)

    def fetch(c):
        source = pl.ds(pl.multiple_of(place(c) * rows, rows), rows)
        side = lax.rem(c, 2)
        return pltpu.make_async_copy(xs.at[:, source, :], x_buf.at[side], x_sems.at[side])

    fetch(0).start()
    squares[...] = jnp.zeros_like(squares)

    def remotes(c, owner):
        return (
            pltpu.make_async_remote_copy(
                src_ref=send_main.at[c], dst_ref=recv_main.at[:, my_rows, :],
                send_sem=main_sems.at[c], recv_sem=main_recv_sems.at[me],
                device_id={"wide": owner}, device_id_type=MESH,
            ),
            pltpu.make_async_remote_copy(
                src_ref=send_rest.at[c], dst_ref=recv_rest.at[my_rows, :],
                send_sem=rest_sems.at[c], recv_sem=rest_recv_sems.at[me],
                device_id={"wide": owner}, device_id_type=MESH,
            ),
        )

    def locals_(c):
        return (
            pltpu.make_async_copy(send_main.at[c], recv_main.at[:, my_rows, :], own_sems.at[0]),
            pltpu.make_async_copy(send_rest.at[c], recv_rest.at[my_rows, :], own_sems.at[1]),
        )

    def dispatch(c):
        owner = place(c)

        @pl.when(owner != me)
        def _():
            for copy in remotes(c, owner):
                copy.start()

        @pl.when(owner == me)
        def _():
            for copy in locals_(c):
                copy.start()

    lane = lax.broadcasted_iota(jnp.int32, (pair_rows, LANES), 1)

    def block(c, carry):
        @pl.when(c + 1 < n)
        def _():
            fetch(c + 1).start()

        fetch(c).wait()
        for k in range(deep):
            high, low = split(x_buf[lax.rem(c, 2), k])
            x_high[:, k * LANES : (k + 1) * LANES] = high
            x_low[:, k * LANES : (k + 1) * LANES] = low
        dot = functools.partial(jnp.dot, preferred_element_type=jnp.float32)
        small = dot(x_low[...], w_high[...]) + dot(x_high[...], w_low[...])
        product = (dot(x_high[...], w_high[...]) + small).reshape(span, pair_rows, -1) * scales[...][None]
        squares[...] = squares[...] + jnp.sum(product * product, axis=0)
        send_main[c] = product[:, :, :full]
        packed = [jnp.zeros((pair_rows, LANES), jnp.float32)] * (span * rest // LANES)
        for s in range(span):
            at, offset = divmod(s * rest, LANES)
            value = product[s, :, full:]
            if offset:
                value = pltpu.roll(value, offset, axis=1)
            if offset + rest > LANES:
                packed[at] = jnp.where(lane >= offset, value, packed[at])
                packed[at + 1] = jnp.where(lane < offset, value, packed[at + 1])
            else:
                packed[at] = jnp.where(lane >= offset, value, packed[at])
        for b, value in enumerate(packed):
            send_rest[c, :, b * LANES : (b + 1) * LANES] = value

        @pl.when(c == 0)
        def _():
            pl.semaphore_wait(barrier, n - 1)

        @pl.when(c > 0)
        def _():
            dispatch(c - 1)

        return carry

    lax.fori_loop(0, n, block, 0)
    dispatch(n - 1)
    total = squares[:, :LANES]
    for b in range(1, squares.shape[1] // LANES):
        total = total + squares[:, b * LANES : (b + 1) * LANES]
    sq_send[...] = total

    def sq_copy(src, dst, j):
        return pltpu.make_async_remote_copy(
            src_ref=sq_send, dst_ref=sq_recv.at[src],
            send_sem=sq_sems.at[j], recv_sem=sq_recv_sems.at[src],
            device_id={"wide": dst}, device_id_type=MESH,
        )

    for copy in remotes(0, place(0)):
        copy.wait_send()
    own_squares = pltpu.make_async_copy(sq_send, sq_recv.at[me], own_sems.at[2])
    own_squares.start()

    def send_squares(j, carry):
        sq_copy(me, lax.rem(me + j, n), j).start()
        return carry

    lax.fori_loop(1, n, send_squares, 0)
    own_squares.wait()

    def finish_sends(c, carry):
        owner = place(c)

        @pl.when(owner != me)
        def _():
            for copy in remotes(c, owner):
                copy.wait_send()

        @pl.when(owner == me)
        def _():
            for copy in locals_(c):
                copy.wait()

        return carry

    lax.fori_loop(1, n, finish_sends, 0)

    def finish(j, carry):
        src = lax.rem(me + j, n)
        rows = pl.ds(pl.multiple_of(src * pair_rows, pair_rows), pair_rows)
        pltpu.make_async_remote_copy(
            src_ref=send_main.at[0], dst_ref=recv_main.at[:, rows, :],
            send_sem=main_sems.at[0], recv_sem=main_recv_sems.at[src],
            device_id={"wide": src}, device_id_type=MESH,
        ).wait_recv()
        pltpu.make_async_remote_copy(
            src_ref=send_rest.at[0], dst_ref=recv_rest.at[rows, :],
            send_sem=rest_sems.at[0], recv_sem=rest_recv_sems.at[src],
            device_id={"wide": src}, device_id_type=MESH,
        ).wait_recv()
        sq_copy(src, src, j).wait_recv()
        sq_copy(me, src, j).wait_send()
        return carry

    lax.fori_loop(1, n, finish, 0)


def unpack_kernel(count, main_ref, rest_ref, sq_ref, out_ref, rms_ref, turned):
    group, pairs, full = main_ref.shape
    rest = out_ref.shape[1] - full
    step = pl.program_id(0)

    @pl.when(step == 0)
    def _():
        for b in range(rest_ref.shape[1] // LANES):
            turned[b * LANES : (b + 1) * LANES, :] = rest_ref[:, b * LANES : (b + 1) * LANES].T
        totals = jnp.sum(sq_ref[...].T, axis=0, keepdims=True)
        rms_ref[...] = jnp.sqrt(totals / count + 1e-06)

    for g in range(group):
        for b in range(full // LANES):
            out_ref[g, b * LANES : (b + 1) * LANES, :] = main_ref[g, :, b * LANES : (b + 1) * LANES].T
        start = pl.multiple_of((step * group + g) * rest, 8)
        out_ref[g, full:, :] = turned[pl.ds(start, rest), :]


def shards(n, half_integrals, pair_list, occupied_energy, virtual_orbitals, tile_order):
    pair_rows, columns, basis = half_integrals.shape
    virtuals = virtual_orbitals.shape[1]
    pairs = n * pair_rows
    span = columns // n
    deep = round_up(basis, LANES)
    broad = round_up(virtuals, LANES)
    full = virtuals // LANES * LANES
    rest = virtuals - full
    rows = span * pair_rows
    group = 4
    flops = 6 * pair_rows * columns * basis * virtuals
    vmem = pl.BlockSpec(memory_space=pltpu.VMEM)
    anywhere = pl.BlockSpec(memory_space=pl.ANY)

    def whole(*shape):
        return pl.BlockSpec(shape, lambda i: (0,) * len(shape))

    tiles = LANES // TILE_S
    xs, w_high, w_low, scales = pl.pallas_call(
        prepare_kernel,
        grid=(columns // LANES,),
        out_shape=(
            jax.ShapeDtypeStruct((deep // LANES, columns * pair_rows, LANES), jnp.float32),
            jax.ShapeDtypeStruct((deep, broad), jnp.bfloat16),
            jax.ShapeDtypeStruct((deep, broad), jnp.bfloat16),
            jax.ShapeDtypeStruct((pair_rows, broad), jnp.float32),
        ),
        in_specs=[
            pl.BlockSpec(memory_space=pltpu.SMEM),
            whole(2, pairs),
            whole(1, occupied_energy.shape[0]),
            pl.BlockSpec((pair_rows, basis, LANES), lambda i: (0, 0, i)),
            whole(basis, virtuals),
        ],
        out_specs=(anywhere, whole(deep, broad), whole(deep, broad), whole(pair_rows, broad)),
        scratch_shapes=[
            pltpu.VMEM((pairs, LANES), jnp.float32),
            pltpu.VMEM((2, deep // LANES, LANES * pair_rows, LANES), jnp.float32),
            pltpu.SMEM(tile_order.shape, jnp.int32),
            pltpu.SemaphoreType.DMA((2, tiles)),
        ],
        compiler_params=pltpu.CompilerParams(vmem_limit_bytes=54 * 1024 * 1024),
        name="prepare",
    )(tile_order, pair_list.T, occupied_energy.reshape(1, -1), jnp.swapaxes(half_integrals, 1, 2), virtual_orbitals)
    recv_main, recv_rest, sq_recv = pl.pallas_call(
        functools.partial(exchange_kernel, n),
        out_shape=(
            jax.ShapeDtypeStruct((span, pairs, full), jnp.float32),
            jax.ShapeDtypeStruct((pairs, span * rest), jnp.float32),
            jax.ShapeDtypeStruct((n, pair_rows, LANES), jnp.float32),
        ),
        in_specs=[anywhere, vmem, vmem, vmem],
        out_specs=(anywhere, anywhere, anywhere),
        scratch_shapes=[
            pltpu.VMEM((2, deep // LANES, rows, LANES), jnp.float32),
            pltpu.VMEM((rows, deep), jnp.bfloat16),
            pltpu.VMEM((rows, deep), jnp.bfloat16),
            pltpu.VMEM((pair_rows, broad), jnp.float32),
            pltpu.VMEM((pair_rows, LANES), jnp.float32),
            pltpu.VMEM((n, span, pair_rows, full), jnp.float32),
            pltpu.VMEM((n, pair_rows, span * rest), jnp.float32),
            pltpu.SemaphoreType.DMA((2,)),
            pltpu.SemaphoreType.DMA((n,)),
            pltpu.SemaphoreType.DMA((n,)),
            pltpu.SemaphoreType.DMA((n,)),
            pltpu.SemaphoreType.DMA((n,)),
            pltpu.SemaphoreType.DMA((n,)),
            pltpu.SemaphoreType.DMA((n,)),
            pltpu.SemaphoreType.DMA((3,)),
        ],
        compiler_params=pltpu.CompilerParams(
            collective_id=0, has_side_effects=True, vmem_limit_bytes=30 * 1024 * 1024
        ),
        cost_estimate=pl.CostEstimate(flops=flops, bytes_accessed=4 * half_integrals.size, transcendentals=0),
        name="exchange",
    )(xs, w_high, w_low, scales)
    out, rms = pl.pallas_call(
        functools.partial(unpack_kernel, columns * virtuals),
        grid=(span // group,),
        out_shape=(
            jax.ShapeDtypeStruct((span, virtuals, pairs), jnp.float32),
            jax.ShapeDtypeStruct((1, pairs), jnp.float32),
        ),
        in_specs=[
            pl.BlockSpec((group, pairs, full), lambda i: (i, 0, 0)),
            pl.BlockSpec((pairs, span * rest), lambda i: (0, 0)),
            pl.BlockSpec((pairs, LANES), lambda i: (0, 0)),
        ],
        out_specs=(
            pl.BlockSpec((group, virtuals, pairs), lambda i: (i, 0, 0)),
            pl.BlockSpec((1, pairs), lambda i: (0, 0)),
        ),
        scratch_shapes=[pltpu.VMEM((span * rest, pairs), jnp.float32)],
        compiler_params=pltpu.CompilerParams(vmem_limit_bytes=20 * 1024 * 1024),
        name="unpack",
    )(recv_main, recv_rest, sq_recv.reshape(pairs, LANES))
    return (jnp.transpose(out, (2, 0, 1)), rms.reshape(-1))


def solution(mesh):
    in_specs = (
        P(("groups", "wide"), None, None),
        P("groups", None),
        P("groups"),
        P("groups", None),
        P(),
    )
    out_specs = (P("groups", "wide", None), P("groups"))
    return jax.shard_map(
        functools.partial(shards, mesh.shape["wide"]),
        mesh=mesh, in_specs=in_specs, out_specs=out_specs, check_vma=False,
    )
```

time: 367 us -> 259 us (0.71)
  Pallas kernels: 0 us -> 252 us
  blocking collectives: 244 us -> 0 us
  local copies, waits for them, and re-layouts: 75.4 us -> 3.24 us
  matrix products: 37.2 us -> 0 us
  starting transfers between devices: 6.32 us -> 0 us
    pallas_call x0 -> x3, Pallas kernels: none -> 252 us  [the longest x1 230 us: shards(): pl.pallas_call(functools.partial(exchange_kernel, n), out_shape=(jax.Shap...]
    unnamed x1 -> x0, blocking collectives: 244 us -> none
    dot_general x1 -> x0, matrix products: 37.2 us -> none  [transform(): jnp.einsum('psr,ra->psa', block, virtual_orbitals, precision=lax.Precisio...]
    unnamed x13 -> x6, local copies, waits for them, and re-layouts: 28.1 us -> 3.24 us
    reshape x1 -> x0, local copies, waits for them, and re-layouts: 12.4 us -> none  [shards(): half_integrals.reshape(pair_rows, tile_order.shape[0], TILE_S, basis)]
    mul x1 -> x0, local copies, waits for them, and re-layouts: 12.3 us -> none  [transform(): return product * scale[:, None, None]]
    gather x1 -> x0, local copies, waits for them, and re-layouts: 11.9 us -> none  [shards(): jnp.take(tiled, tile_order, axis=1).reshape(pair_rows, columns, basis)]
    all_to_all x1 -> x0, local copies, waits for them, and re-layouts: 9.78 us -> none  [shards(): lax.all_to_all(local, 'wide', split_axis=1, concat_axis=0, tiled=True)]
  transfers between devices with their start and end apart: 1 -> 0, of which waited for: 0 -> 0; matrix products, arithmetic and copies ran while one was open for 0% -> 0% of each run, Pallas kernels for 0% -> 0%
where the time goes in v1:
time: 259 us; the launch traced here: 256 us
  Pallas kernels  252 us (97%)
  local copies, waits for them, and re-layouts  3.24 us (1%)
    pallas_call x1, Pallas kernels, shards(): pl.pallas_call(functools.partial(exchange_kernel, n), out_shape=(jax.Shap...  230 us
    pallas_call x1, Pallas kernels, shards(): pl.pallas_call(prepare_kernel, grid=(columns // LANES,), out_shape=(jax.S...  15.5 us
    pallas_call x1, Pallas kernels, shards(): pl.pallas_call(functools.partial(unpack_kernel, columns * virtuals), grid...  6.36 us

profile of v1, /device:TPU:16, one launch (start us, length us, event | category | flops | bytes accessed | tf_op | source)
XLA Modules:
  0.0 255.9 jit_solution(9250910526924960976)
XLA Ops:
  0.6 15.5 %prepare.1 = (f32[7,4096,128]{2,1,0:T(8,128)}, bf16[896,640]{1,0:T(8,128)(2,1)}, bf16[896,640]{1,0:T(8,128)(2,1)}, f32[8,640]{1,0:T(8,128)}) custom-call(s32[64]{0:T(128)} %order_ref.1, s32[2,128]{1,0:T(2,128)} %bitcast.8, f32[1,200]{1,0:T(1,128)} %bitcast.9, f32[8,800,512]{2,1,0:T(8,128)} %bitcast.7, f32[800,600]{1,0:T(8,128)} %w_ref.1), custom_call_target="tpu_custom_call" | custom-call | tf_op jit(solution)/shard_map/prepare/pallas_call | solution.py:303
  16.1 0.0 copy-start
  16.1 1.2 copy-done
  17.4 0.0 copy-start.1
  17.4 1.3 copy-done.1
  18.6 0.0 copy-start.2
  18.6 0.7 copy-done.2
  19.4 230.2 %exchange.1 = (f32[32,128,512]{2,1,0:T(8,128)S(1)}, f32[128,2816]{1,0:T(8,128)S(1)}, f32[16,8,128]{2,1,0:T(8,128)S(1)}) custom-call(f32[7,4096,128]{2,1,0:T(8,128)} %get-tuple-element.11.xs, bf16[896,640]{1,0:T(8,128)(2,1)S(1)} %copy-done, bf16[896,640]{1,0:T(8,128)(2,1)S(1)} %copy-done.1, f32[8,640]{1,0:T(8,128)S(1)} %copy-done.2), custom_call_target="tpu_custom_call" | custom-call | flops 11796480000 | bytes 13107200 | tf_op jit(solution)/shard_map/exchange/pallas_call | solution.py:329
  249.6 6.4 %unpack.1 = (f32[32,600,128]{2,1,0:T(8,128)}, f32[1,128]{1,0:T(1,128)}) custom-call(f32[32,128,512]{2,1,0:T(8,128)S(1)} %get-tuple-element.15.main_ref, f32[128,2816]{1,0:T(8,128)S(1)} %get-tuple-element.16.rest_ref, f32[128,128]{1,0:T(8,128)S(1)} %bitcast.6), custom_call_target="tpu_custom_call" | custom-call | tf_op jit(solution)/shard_map/unpack/pallas_call | solution.py:361
Async XLA Ops:
  16.1 1.3 copy-start
  17.4 1.3 copy-start.1
  18.6 0.7 copy-start.2

commit v2 on v1

--- a/solution.py
+++ b/solution.py
@@ -170,6 +170,15 @@
             high, low = split(x_buf[lax.rem(c, 2), k])
             x_high[:, k * LANES : (k + 1) * LANES] = high
             x_low[:, k * LANES : (k + 1) * LANES] = low
+
+        @pl.when(c == 1)
+        def _():
+            pl.semaphore_wait(barrier, n - 1)
+
+        @pl.when(c > 0)
+        def _():
+            dispatch(c - 1)
+
         dot = functools.partial(jnp.dot, preferred_element_type=jnp.float32)
         small = dot(x_low[...], w_high[...]) + dot(x_high[...], w_low[...])
         product = (dot(x_high[...], w_high[...]) + small).reshape(span, pair_rows, -1) * scales[...][None]
@@ -189,14 +198,6 @@
         for b, value in enumerate(packed):
             send_rest[c, :, b * LANES : (b + 1) * LANES] = value
 
-        @pl.when(c == 0)
-        def _():
-            pl.semaphore_wait(barrier, n - 1)
-
-        @pl.when(c > 0)
-        def _():
-            dispatch(c - 1)
-
         return carry
 
     lax.fori_loop(0, n, block, 0)
@@ -323,9 +324,9 @@
             pltpu.SMEM(tile_order.shape, jnp.int32),
             pltpu.SemaphoreType.DMA((2, tiles)),
         ],
-        compiler_params=pltpu.CompilerParams(vmem_limit_bytes=54 * 1024 * 1024),
+        compiler_params=pltpu.CompilerParams(vmem_limit_bytes=28 * 1024 * 1024),
         name="prepare",
-    )(tile_order, pair_list.T, occupied_energy.reshape(1, -1), jnp.swapaxes(half_integrals, 1, 2), virtual_orbitals)
+    )(tile_order, pair_list.T, occupied_energy.reshape(1, -1), pltpu.with_memory_space_constraint(jnp.swapaxes(half_integrals, 1, 2), pltpu.HBM), virtual_orbitals)
     recv_main, recv_rest, sq_recv = pl.pallas_call(
         functools.partial(exchange_kernel, n),
         out_shape=(
@@ -353,7 +354,7 @@
             pltpu.SemaphoreType.DMA((3,)),
         ],
         compiler_params=pltpu.CompilerParams(
-            collective_id=0, has_side_effects=True, vmem_limit_bytes=30 * 1024 * 1024
+            collective_id=0, has_side_effects=True, vmem_limit_bytes=20 * 1024 * 1024
         ),
         cost_estimate=pl.CostEstimate(flops=flops, bytes_accessed=4 * half_integrals.size, transcendentals=0),
         name="exchange",

time: 259 us -> 254 us (0.981)
  Pallas kernels: 252 us -> 247 us
    pallas_call x1, Pallas kernels: 15.5 us -> 11.7 us  [shards(): pl.pallas_call(prepare_kernel, grid=(columns // LANES,), out_shape=(jax.S...]
where the time goes in v2:
time: 254 us; the launch traced here: 251 us
  Pallas kernels  247 us (97%)
  local copies, waits for them, and re-layouts  3.58 us (1%)
    pallas_call x1, Pallas kernels, shards(): pl.pallas_call(functools.partial(exchange_kernel, n), out_shape=(jax.Shap...  229 us
    pallas_call x1, Pallas kernels, shards(): pl.pallas_call(prepare_kernel, grid=(columns // LANES,), out_shape=(jax.S...  11.7 us
    pallas_call x1, Pallas kernels, shards(): pl.pallas_call(functools.partial(unpack_kernel, columns * virtuals), grid...  6.36 us

profile of v2, /device:TPU:16, one launch (start us, length us, event | category | flops | bytes accessed | tf_op | source)
XLA Modules:
  0.0 251.2 jit_solution(15625946934485084664)
XLA Ops:
  0.6 0.0 copy-start
  0.6 1.6 copy-done
  2.2 0.0 copy-start.1
  2.2 0.7 copy-done.1
  2.9 0.0 copy-start.2
  2.9 0.7 copy-done.2
  3.6 0.0 copy-start.3
  3.6 0.7 copy-done.3
  4.2 11.7 %prepare.1 = (f32[7,4096,128]{2,1,0:T(8,128)S(1)}, bf16[896,640]{1,0:T(8,128)(2,1)S(1)}, bf16[896,640]{1,0:T(8,128)(2,1)S(1)}, f32[8,640]{1,0:T(8,128)S(1)}) custom-call(s32[64]{0:T(128)S(1)} %copy-done.3, s32[2,128]{1,0:T(2,128)S(1)} %bitcast.7, f32[1,200]{1,0:T(1,128)S(1)} %bitcast.8, f32[8,800,512]{2,1,0:T(8,128)} %bitcast.9, f32[800,600]{1,0:T(8,128)S(1)} %copy-done), custom_call_target="tpu_custom_call" | custom-call | tf_op jit(solution)/shard_map/prepare/pallas_call | solution.py:304
  15.9 229.0 %exchange.1 = (f32[32,128,512]{2,1,0:T(8,128)S(1)}, f32[128,2816]{1,0:T(8,128)S(1)}, f32[16,8,128]{2,1,0:T(8,128)S(1)}) custom-call(f32[7,4096,128]{2,1,0:T(8,128)S(1)} %get-tuple-element.11.xs, bf16[896,640]{1,0:T(8,128)(2,1)S(1)} %get-tuple-element.12.w_high, bf16[896,640]{1,0:T(8,128)(2,1)S(1)} %get-tuple-element.13.w_low, ...), custom_call_target="tpu_custom_call" | custom-call | flops 11796480000 | bytes 13107200 | tf_op jit(solution)/shard_map/exchange/pallas_call | solution.py:330
  244.9 6.4 %unpack.1 = (f32[32,600,128]{2,1,0:T(8,128)}, f32[1,128]{1,0:T(1,128)}) custom-call(f32[32,128,512]{2,1,0:T(8,128)S(1)} %get-tuple-element.15.main_ref, f32[128,2816]{1,0:T(8,128)S(1)} %get-tuple-element.16.rest_ref, f32[128,128]{1,0:T(8,128)S(1)} %bitcast.6), custom_call_target="tpu_custom_call" | custom-call | tf_op jit(solution)/shard_map/unpack/pallas_call | solution.py:362
Async XLA Ops:
  0.6 1.6 copy-start
  2.2 0.7 copy-start.1
  2.9 0.7 copy-start.2
  3.6 0.7 copy-start.3
